TPU v7x, 256 devices: a 4x2x16 block of a 4x16x16 slice. The times are simulated.
256 devices in a mesh: groups: 2 (over y), grid: 32 (over z, core), depth: 4 (over x).
Axes of the slice: x: 4, y: 2, z: 16, core: 2. Of those that a mesh axis runs over, the one named last changes fastest.
The devices are a block of a 4x16x16 slice.
Arguments:
- tokens: bfloat16 [4096, 4096], P(('groups', 'grid'), 'depth'), parts along dimension 0, may hold values from -6 to 6
- gate_weight: bfloat16 [4096, 14336], P('depth', 'grid'), may hold values from -0.09375 to 0.09375
- up_weight: bfloat16 [4096, 14336], P('depth', 'grid'), may hold values from -0.09375 to 0.09375
- down_weight: bfloat16 [14336, 4096], P('grid', 'depth'), may hold values from -0.046875 to 0.046875
Outputs:
- mixed: bfloat16 [4096, 4096], P(('groups', 'grid'), 'depth'), parts along dimension 0
There are 2 independent parts, one for each index of `groups`. A program takes and returns all parts, laid end to end along the dimension named above; an argument that names none is the same for every part. Nothing has to cross between parts.
All inputs are finite; a program needn't handle non-finite values.
Results may differ from a plain program's by a relative error of at most 0.0049.
Values may be sent and summed in bfloat16 or wider, within the bound.
A program may use at most 64 MiB of HBM per device.

v0:
```python
import jax
import jax.numpy as jnp
from jax import lax
from jax.sharding import Mesh
from jax.sharding import PartitionSpec as P

GRID = ("grid_0", "grid_1")
GROUPS_GRID = ("groups", "grid_0", "grid_1")


def joined_along(blocks, dim):
    shape = list(blocks.shape[1:])
    shape[dim] *= blocks.shape[0]
    return jnp.moveaxis(blocks, 0, dim).reshape(shape)


def sent_to_all(value, axis):
    copies = jnp.broadcast_to(value, (lax.axis_size(axis), *value.shape))
    return lax.all_to_all(copies, axis, split_axis=0, concat_axis=0, tiled=True)


def gathered_copies(value, axis, dim):
    return joined_along(sent_to_all(value, axis), dim)


def own_block(blocks, axes, sequence):
    shape = [lax.axis_size(a) for a in axes]
    blocks = blocks.reshape(*shape, *blocks.shape[1:])
    blocks = blocks.transpose(*sequence, *range(len(axes), blocks.ndim))
    blocks = blocks.reshape(-1, *blocks.shape[len(axes) :])
    for k in sequence:
        blocks = lax.psum_scatter(blocks, axes[k], scatter_dimension=0, tiled=True)
    return blocks[0]


def cut_along(value, dim, length):
    shape = value.shape
    blocks = value.reshape(*shape[:dim], length, shape[dim] // length, *shape[dim + 1 :])
    return jnp.moveaxis(blocks, dim, 0)


def scatter_axes(value, axes, sequence, dim):
    length = lax.axis_size(axes)
    return own_block(cut_along(value, dim, length), axes, sequence)


def body(tokens, gate_weight, up_weight, down_weight):
    grid_size = lax.axis_size(GRID)
    block_rows = tokens.shape[0]
    total_rows = block_rows * grid_size
    width_share = gate_weight.shape[1]
    stacked = jnp.concatenate([gate_weight, up_weight], axis=1)
    pre_act = jnp.dot(
        lax.all_gather(tokens, GRID, axis=0, tiled=True),
        stacked,
        preferred_element_type=jnp.float32,
    )
    blocked = pre_act.reshape(grid_size, block_rows, 2 * width_share)
    summed = lax.psum_scatter(blocked, "depth", scatter_dimension=1, tiled=True)
    hidden = gathered_copies(
        (jax.nn.silu(summed[..., :width_share]) * summed[..., width_share:]).astype(jnp.bfloat16),
        "depth",
        1,
    ).reshape(total_rows, width_share)
    return scatter_axes(
        jnp.dot(hidden, down_weight, preferred_element_type=jnp.float32), GRID, (1, 0), 0
    ).astype(jnp.bfloat16)


def solution(mesh):
    torus = Mesh(
        mesh.devices.reshape(mesh.shape["groups"], 16, 2, mesh.shape["depth"]),
        ("groups", "grid_0", "grid_1", "depth"),
    )
    placed = (P(GROUPS_GRID, "depth"), P("depth", GRID), P("depth", GRID), P(GRID, "depth"))
    return jax.shard_map(
        body, mesh=torus, in_specs=placed, out_specs=P(GROUPS_GRID, "depth"), check_vma=False
    )
```

profile of v0, /device:TPU:34, one launch (start us, length us, event | category | flops | bytes accessed | tf_op | source)
XLA Modules:
  0.0 342.8 jit_solution(1183751066836995780)
XLA Ops:
  6.5 0.0 copy-start
  6.6 0.0 all-gather.2.cloned.1.call-start
  6.6 0.7 all-gather.2.cloned.1.call-update
  7.3 0.1 reduce-scatter.4.cloned.1.call-start
  7.4 87.2 %all-gather.2.cloned.1.call-done = bf16[2048,1024]{1,0:T(8,128)(2,1)} async-done(((bf16[64,1024]{1,0:T(8,128)(2,1)}), bf16[2048,1024]{1,0:T(8,128)(2,1)}) %all-gather.2.cloned.1.call-update) | async-done | bytes 4194320 | tf_op jit(solution)/shard_map/all_gather | solution.py:54
  94.6 9.7 %convolution_bitcast_fusion = f32[2048,896]{0,1:T(8,128)} fusion(bf16[2048,1024]{1,0:T(8,128)(2,1)} %all-gather.2.cloned.1.call-done, bf16[1024,448]{0,1:T(8,128)(2,1)} %param.6, bf16[1024,448]{0,1:T(8,128)(2,1)} %param.5), kind=kOutput, calls=%fused_computation | convolution fusion | flops 3761766400 | bytes 13369344 | tf_op jit(solution)/shard_map/dot_general | solution.py:53
  104.3 8.6 %copy.8 = f32[2048,896]{1,0:T(8,128)} copy(f32[2048,896]{0,1:T(8,128)} %convolution_bitcast_fusion) | data formatting | bytes 14680064 | tf_op jit(solution)/shard_map/dot_general | solution.py:53
  112.9 0.1 reduce-scatter.4.cloned.1.call-update
  112.9 0.1 reduce-scatter.6.cloned.1.call-start
  113.0 74.8 %reduce-scatter.4.cloned.1.call-done = f32[32,16,896]{2,1,0:T(8,128)} async-done(((f32[32,64,896]{2,1,0:T(8,128)}), f32[32,16,896]{2,1,0:T(8,128)}) %reduce-scatter.4.cloned.1.call-update) | async-done | bytes 1835024 | tf_op jit(solution)/shard_map/reduce_scatter | solution.py:59
  187.7 1.9 fusion.3
  189.7 0.3 broadcast_in_dim.3
  190.0 29.4 %all_to_all.5 = bf16[4,32,16,448]{3,2,1,0:T(8,128)(2,1)S(1)} all-to-all(bf16[4,32,16,448]{3,2,1,0:T(8,128)(2,1)S(1)} %broadcast_in_dim.3), channel_id=1, replica_groups=mesh['groups'=2,'grid_0'=16,'grid_1'=2,'depth'=4] {'depth'}, dimensions={0} | all-to-all | bytes 3670016 | tf_op jit(solution)/shard_map/all_to_all | solution.py:19
  219.4 0.2 copy.9
  219.6 0.0 copy-done
  219.6 2.4 convolution_bitcast_fusion.1
  222.0 4.1 %copy.10 = f32[2,16,64,1024]{3,2,1,0:T(8,128)} copy(f32[2,16,64,1024]{3,2,0,1:T(8,128)S(1)} %convolution_bitcast_fusion.1) | data formatting | bytes 16777216 | tf_op jit(solution)/shard_map/transpose | solution.py:29
  226.0 0.1 reduce-scatter.6.cloned.1.call-update
  226.1 0.1 reduce-scatter.8.cloned.1.call-start
  226.2 25.8 %reduce-scatter.6.cloned.1.call-done = f32[16,64,1024]{2,1,0:T(8,128)} async-done(((f32[32,64,1024]{2,1,0:T(8,128)}), f32[16,64,1024]{2,1,0:T(8,128)}) %reduce-scatter.6.cloned.1.call-update) | async-done | bytes 4194320 | tf_op jit(solution)/shard_map/reduce_scatter | solution.py:32
  252.0 0.1 reduce-scatter.8.cloned.1.call-update
  252.0 82.6 %reduce-scatter.8.cloned.1.call-done = f32[1,64,1024]{2,1,0:T(8,128)} async-done(((f32[16,64,1024]{2,1,0:T(8,128)}), f32[1,64,1024]{2,1,0:T(8,128)}) %reduce-scatter.8.cloned.1.call-update) | async-done | bytes 262160 | tf_op jit(solution)/shard_map/reduce_scatter | solution.py:32
  334.6 1.6 convert_bitcast_fusion
Async XLA Ops:
  6.5 213.1 %copy-start = (bf16[448,1024]{1,0:T(8,128)(2,1)S(1)}, bf16[448,1024]{1,0:T(8,128)(2,1)}, u32[]{:S(2)}) copy-start(bf16[448,1024]{1,0:T(8,128)(2,1)} %param.7) | copy-start | bytes 2752516
  6.6 88.0 %all-gather.2.cloned.1.call-start = ((), (), s32[]{:S(2)}) async-start(), calls=%async_computation.4 | async-start | bytes 4325376 | tf_op jit(solution)/shard_map/all_gather | solution.py:54
  7.3 180.4 %reduce-scatter.4.cloned.1.call-start = ((), (), s32[]{:S(2)}) async-start(), calls=%async_computation.5 | async-start | bytes 9175040 | tf_op jit(solution)/shard_map/reduce_scatter | solution.py:59
  112.9 139.1 %reduce-scatter.6.cloned.1.call-start = ((), (), s32[]{:S(2)}) async-start(), calls=%async_computation.6 | async-start | bytes 12582912 | tf_op jit(solution)/shard_map/reduce_scatter | solution.py:32
  226.1 108.5 %reduce-scatter.8.cloned.1.call-start = ((), (), s32[]{:S(2)}) async-start(), calls=%async_computation.7 | async-start | bytes 4456448 | tf_op jit(solution)/shard_map/reduce_scatter | solution.py:32
Sparse Core Ops, SparseCore 0:
  9.2 85.3 all-gather.1
  113.0 74.6 reduce-scatter.3
  226.2 25.7 reduce-scatter.5
  254.4 80.1 reduce-scatter.7
where the time goes:
time: 343 us
  waiting for transfers between devices  271 us (79%)
  blocking collectives  29.4 us (9%)
  between operations  13.2 us (4%)
  local copies, waits for them, and re-layouts  13.1 us (4%)
  matrix products  12.1 us (4%)
  other arithmetic  3.57 us (1%)
    reduce_scatter x2, waiting for transfers between devices, own_block(): blocks = lax.psum_scatter(blocks, axes[k], scatter_dimension=0, tiled=True)  108 us
    all_gather x1, waiting for transfers between devices, body(): lax.all_gather(tokens, GRID, axis=0, tiled=True)  87.2 us
    reduce_scatter x1, waiting for transfers between devices, body(): summed = lax.psum_scatter(blocked, 'depth', scatter_dimension=1, tiled=True)  74.8 us
    all_to_all x1, blocking collectives, sent_to_all(): return lax.all_to_all(copies, axis, split_axis=0, concat_axis=0, tiled=True)  29.4 us
    dot_general x1, matrix products, body(): jnp.dot(lax.all_gather(tokens, GRID, axis=0, tiled=True), stacked, prefer...  9.7 us
    dot_general x1, local copies, waits for them, and re-layouts, body(): jnp.dot(lax.all_gather(tokens, GRID, axis=0, tiled=True), stacked, prefer...  8.59 us
  transfers between devices with their start and end apart: 4, of which 4 were waited for; matrix products, arithmetic and copies ran while one was open for 0% of the time, Pallas kernels for 0%

commit v1 on v0

--- a/solution.py
+++ b/solution.py
@@ -51,7 +51,9 @@
     width_share = gate_weight.shape[1]
     stacked = jnp.concatenate([gate_weight, up_weight], axis=1)
     pre_act = jnp.dot(
-        lax.all_gather(tokens, GRID, axis=0, tiled=True),
+        jnp.concatenate(
+            lax.all_to_all(jnp.stack([tokens] * lax.axis_size(GRID)), GRID, 0, 0), axis=0
+        ),
         stacked,
         preferred_element_type=jnp.float32,
     )

time: 343 us -> 463 us (1.35)
  blocking collectives: 29.4 us -> 244 us
  waiting for transfers between devices: 271 us -> 179 us
    all_to_all x0 -> x1, blocking collectives: none -> 215 us  [body(): lax.all_to_all(jnp.stack([tokens] * lax.axis_size(GRID)), GRID, 0, 0)]
    all_gather x1 -> x0, waiting for transfers between devices: 87.2 us -> none  [body(): lax.all_gather(tokens, GRID, axis=0, tiled=True)]
    reduce_scatter x1, waiting for transfers between devices: 74.8 us -> 70 us  [body(): summed = lax.psum_scatter(blocked, 'depth', scatter_dimension=1, tiled=True)]
  transfers between devices with their start and end apart: 4 -> 3, of which waited for: 4 -> 3; matrix products, arithmetic and copies ran while one was open for 0% -> 0% of each run, Pallas kernels for 0% -> 0%
where the time goes in v1:
time: 463 us
  blocking collectives  244 us (53%)
  waiting for transfers between devices  179 us (39%)
  local copies, waits for them, and re-layouts  14.7 us (3%)
  between operations  13.2 us (3%)
  matrix products  8.37 us (2%)
    all_to_all x1, blocking collectives, body(): lax.all_to_all(jnp.stack([tokens] * lax.axis_size(GRID)), GRID, 0, 0)  215 us
    reduce_scatter x2, waiting for transfers between devices, own_block(): blocks = lax.psum_scatter(blocks, axes[k], scatter_dimension=0, tiled=True)  109 us
    reduce_scatter x1, waiting for transfers between devices, body(): summed = lax.psum_scatter(blocked, 'depth', scatter_dimension=1, tiled=True)  70 us
    all_to_all x1, blocking collectives, sent_to_all(): return lax.all_to_all(copies, axis, split_axis=0, concat_axis=0, tiled=True)  29.4 us
  transfers between devices with their start and end apart: 3, of which 3 were waited for; matrix products, arithmetic and copies ran while one was open for 0% of the time, Pallas kernels for 0%

profile of v1, /device:TPU:34, one launch (start us, length us, event | category | flops | bytes accessed | tf_op | source)
XLA Modules:
  0.0 462.8 jit_solution(16266222521219105657)
XLA Ops:
  6.5 0.0 copy-start
  6.6 0.0 reduce-scatter.4.cloned.1.call-start
  6.6 1.5 stack.2
  8.1 0.0 copy-start.1
  8.1 0.0 copy-start.2
  8.1 214.8 %all_to_all.10 = bf16[32,64,1024]{2,1,0:T(8,128)(2,1)S(1)} all-to-all(bf16[32,64,1024]{2,1,0:T(8,128)(2,1)S(1)} %stack.2), channel_id=1, replica_groups=mesh['groups'=2,'grid_0'=16,'grid_1'=2,'depth'=4] {'grid_0','grid_1'}, dimensions={0} | all-to-all | bytes 8388608 | tf_op jit(solution)/shard_map/all_to_all | solution.py:55
  222.9 0.0 copy-done.1
  222.9 0.0 copy-done.2
  222.9 6.0 %convolution_bitcast_fusion = f32[2048,896]{0,1:T(8,128)} fusion(bf16[2048,1024]{1,0:T(8,128)(2,1)S(1)} %bitcast.21, bf16[1024,448]{0,1:T(8,128)(2,1)S(1)} %copy-done.1, bf16[1024,448]{0,1:T(8,128)(2,1)S(1)} %copy-done.2), kind=kOutput, calls=%fused_computation | convolution fusion | flops 3761766400 | bytes 13369344 | tf_op jit(solution)/shard_map/dot_general | solution.py:53
  228.9 8.6 %copy.8 = f32[2048,896]{1,0:T(8,128)} copy(f32[2048,896]{0,1:T(8,128)} %convolution_bitcast_fusion) | data formatting | bytes 14680064 | tf_op jit(solution)/shard_map/dot_general | solution.py:53
  237.5 0.1 reduce-scatter.4.cloned.1.call-update
  237.6 0.1 reduce-scatter.6.cloned.1.call-start
  237.6 70.0 %reduce-scatter.4.cloned.1.call-done = f32[32,16,896]{2,1,0:T(8,128)} async-done(((f32[32,64,896]{2,1,0:T(8,128)}), f32[32,16,896]{2,1,0:T(8,128)}) %reduce-scatter.4.cloned.1.call-update) | async-done | bytes 1835024 | tf_op jit(solution)/shard_map/reduce_scatter | solution.py:61
  307.7 1.9 fusion.3
  309.6 0.3 broadcast_in_dim.3
  309.9 29.4 %all_to_all.11 = bf16[4,32,16,448]{3,2,1,0:T(8,128)(2,1)S(1)} all-to-all(bf16[4,32,16,448]{3,2,1,0:T(8,128)(2,1)S(1)} %broadcast_in_dim.3), channel_id=1, replica_groups=mesh['groups'=2,'grid_0'=16,'grid_1'=2,'depth'=4] {'depth'}, dimensions={0} | all-to-all | bytes 3670016 | tf_op jit(solution)/shard_map/all_to_all | solution.py:19
  339.3 0.2 copy.9
  339.5 0.0 copy-done
  339.5 2.3 convolution_bitcast_fusion.1
  341.9 4.1 copy.10
  346.0 0.1 reduce-scatter.6.cloned.1.call-update
  346.0 0.1 reduce-scatter.8.cloned.1.call-start
  346.1 25.8 %reduce-scatter.6.cloned.1.call-done = f32[16,64,1024]{2,1,0:T(8,128)} async-done(((f32[32,64,1024]{2,1,0:T(8,128)}), f32[16,64,1024]{2,1,0:T(8,128)}) %reduce-scatter.6.cloned.1.call-update) | async-done | bytes 4194320 | tf_op jit(solution)/shard_map/reduce_scatter | solution.py:32
  371.9 0.1 reduce-scatter.8.cloned.1.call-update
  371.9 82.7 %reduce-scatter.8.cloned.1.call-done = f32[1,64,1024]{2,1,0:T(8,128)} async-done(((f32[16,64,1024]{2,1,0:T(8,128)}), f32[1,64,1024]{2,1,0:T(8,128)}) %reduce-scatter.8.cloned.1.call-update) | async-done | bytes 262160 | tf_op jit(solution)/shard_map/reduce_scatter | solution.py:32
  454.7 1.6 convert_bitcast_fusion
Async XLA Ops:
  6.5 333.0 %copy-start = (bf16[448,1024]{1,0:T(8,128)(2,1)S(1)}, bf16[448,1024]{1,0:T(8,128)(2,1)}, u32[]{:S(2)}) copy-start(bf16[448,1024]{1,0:T(8,128)(2,1)} %param.7) | copy-start | bytes 2752516
  6.6 301.1 %reduce-scatter.4.cloned.1.call-start = ((), (), s32[]{:S(2)}) async-start(), calls=%async_computation.5 | async-start | bytes 9175040 | tf_op jit(solution)/shard_map/reduce_scatter | solution.py:61
  8.1 214.8 %copy-start.1 = (bf16[1024,448]{0,1:T(8,128)(2,1)S(1)}, bf16[1024,448]{0,1:T(8,128)(2,1)}, u32[]{:S(2)}) copy-start(bf16[1024,448]{0,1:T(8,128)(2,1)} %param.6) | copy-start | bytes 2752516
  8.1 214.8 %copy-start.2 = (bf16[1024,448]{0,1:T(8,128)(2,1)S(1)}, bf16[1024,448]{0,1:T(8,128)(2,1)}, u32[]{:S(2)}) copy-start(bf16[1024,448]{0,1:T(8,128)(2,1)} %param.5) | copy-start | bytes 2752516
  237.6 134.3 %reduce-scatter.6.cloned.1.call-start = ((), (), s32[]{:S(2)}) async-start(), calls=%async_computation.6 | async-start | bytes 12582912 | tf_op jit(solution)/shard_map/reduce_scatter | solution.py:32
  346.0 108.7 %reduce-scatter.8.cloned.1.call-start = ((), (), s32[]{:S(2)}) async-start(), calls=%async_computation.7 | async-start | bytes 4456448 | tf_op jit(solution)/shard_map/reduce_scatter | solution.py:32
Sparse Core Ops, SparseCore 0:
  237.7 69.9 reduce-scatter.3
  346.1 25.6 reduce-scatter.5
  374.5 80.1 reduce-scatter.7
